TPU v7x, 256 devices: a whole 4x4x8 slice. The times are simulated.
256 devices in a mesh: gx: 8 (over x, core), gy: 4 (over z_hi), gz: 8 (over z_lo, y).
Axes of the slice: x: 4, y: 4, z: 8 (z_hi: 4, z_lo: 2; z = z_hi * 2 + z_lo), core: 2. Of those that a mesh axis runs over, the one named last changes fastest.
Arguments:
- hidden_rows: bfloat16 [4096, 16384], P(('gx', 'gy'), 'gz'), may hold values from -2000 to 2000
- norm_gain: bfloat16 [16384], P('gz'), may hold values from 0.5 to 1.5
- w_query: bfloat16 [16384, 16384], P('gz', ('gx', 'gy')), may hold values from -0.046875 to 0.046875
- w_keyval: bfloat16 [16384, 2048], P('gz', ('gx', 'gy')), may hold values from -0.046875 to 0.046875
- positions: int32 [4096], P('gz'), may hold values from 0 to 1023, as said below
- keyval_order: int32 [8], replicated, may hold values from 0 to 7, each once
Outputs:
- queries: bfloat16 [4096, 16384], P('gz', ('gx', 'gy'))
- keyval_owned: bfloat16 [8, 4096, 256], P('gy', 'gz')
Inputs may be any that keep to these rules, and one draw needn't show every extreme that they name: `positions`: each token's position within its packed document: 0 where a document starts, else one more than the previous token's; a document holds at most 1024 tokens. `keyval_order`: each head once.
All inputs are finite; a program needn't handle non-finite values.
Results may differ from a plain program's by a relative error of at most 0.0066.
Values may be sent and summed in bfloat16 or wider, within the bound.
A program may use at most 128 MiB of HBM per device.

v0:
```python
import math
import jax
import jax.numpy as jnp
from jax import lax
from jax.sharding import PartitionSpec as P

D = 16384
KVH = 8
HD = 128
rope_base = 500000.0
norm_eps = 1e-05


def from_everyone(value, axis):
    copies = jnp.broadcast_to(value, (lax.axis_size(axis), *value.shape))
    return lax.all_to_all(copies, axis, split_axis=0, concat_axis=0, tiled=True)


def taken_together(value, axis):
    everything = from_everyone(value, axis)
    return jnp.sum(everything, axis=0)


def in_blocks(value, dim, count):
    before, after = (value.shape[:dim], value.shape[dim + 1 :])
    return jnp.moveaxis(value.reshape(*before, count, -1, *after), dim, 0)


def summed_on_arrival(value, axis, dim):
    count = lax.axis_size(axis)
    blocks = lax.all_to_all(in_blocks(value, dim, count), axis, 0, 0, tiled=True)
    return jnp.sum(blocks.astype(jnp.float32), axis=0)


def rotate_pairs(values, position_ids, col_start, keys_only):
    row_total, col_width = values.shape
    pair_col = col_start + 2 * jnp.arange(col_width // 2, dtype=jnp.int32)
    within = pair_col % HD
    inv_freq = jnp.exp((within // 2).astype(jnp.float32) * (-2.0 * math.log(rope_base) / HD))
    angles = position_ids.astype(jnp.float32)[:, None] * inv_freq[None, :]
    cosines = jnp.cos(angles)
    sine_part = jnp.sin(angles)
    paired = values.reshape(row_total, col_width // 2, 2)
    even_part = paired[..., 0]
    odd_part = paired[..., 1]
    rotated = jnp.stack(
        [even_part * cosines - odd_part * sine_part, even_part * sine_part + odd_part * cosines],
        axis=-1,
    )
    if keys_only:
        is_key = (pair_col // HD % 2 == 0)[None, :, None]
        rotated = jnp.where(is_key, rotated, paired)
    return rotated.reshape(row_total, col_width)


def body(hidden_rows, norm_gain, w_query, w_keyval, positions, keyval_order):
    widened_gain = norm_gain.astype(jnp.float32)
    widened = hidden_rows.astype(jnp.float32)
    factor = lax.rsqrt(taken_together(jnp.sum(widened * widened, axis=1), "gz") / D + norm_eps)
    normed_rows = (
        hidden_rows.astype(jnp.float32) * factor[:, None] * widened_gain[None, :]
    ).astype(jnp.bfloat16)
    query_width = w_query.shape[1]
    keyval_width = w_keyval.shape[1]
    group_size = lax.axis_size("gy")
    gathered = lax.all_gather(normed_rows, ("gx", "gy"), axis=0, tiled=True)
    query_sum = summed_on_arrival(
        jnp.dot(gathered, w_query, preferred_element_type=jnp.float32).astype(jnp.bfloat16), "gz", 0
    )
    keyval_sum = summed_on_arrival(
        jnp.dot(gathered, w_keyval, preferred_element_type=jnp.float32).astype(jnp.bfloat16),
        "gz",
        0,
    )
    col_index = lax.axis_index("gx") * group_size + lax.axis_index("gy")
    queries = rotate_pairs(query_sum, positions, col_index * query_width, False).astype(
        jnp.bfloat16
    )
    keyval_part = rotate_pairs(keyval_sum, positions, col_index * keyval_width, True).astype(
        jnp.bfloat16
    )
    keyval_all = lax.all_gather(keyval_part, ("gx", "gy"), axis=1, tiled=True)
    slot_count = KVH // group_size
    first_slot = lax.axis_index("gy") * slot_count
    keyval_heads = keyval_all.reshape(keyval_all.shape[0], KVH, 2 * HD)
    wanted = lax.dynamic_slice_in_dim(keyval_order, first_slot, slot_count, 0)
    selector = (wanted[:, None] == jnp.arange(KVH, dtype=jnp.int32)[None, :]).astype(jnp.bfloat16)
    keyval_owned = jnp.einsum(
        "sh,rhc->src", selector, keyval_heads, preferred_element_type=jnp.float32
    ).astype(jnp.bfloat16)
    return (queries, keyval_owned)


def solution(mesh):
    in_specs = (
        P(("gx", "gy"), "gz"),
        P("gz"),
        P("gz", ("gx", "gy")),
        P("gz", ("gx", "gy")),
        P("gz"),
        P(),
    )
    out_specs = (P("gz", ("gx", "gy")), P("gy", "gz", None))
    return jax.shard_map(body, mesh=mesh, in_specs=in_specs, out_specs=out_specs, check_vma=False)
```

profile of v0, /device:TPU:1, one launch (start us, length us, event | category | flops | bytes accessed | tf_op | source)
XLA Modules:
  0.0 268.1 jit_solution(16777390107375378753)
XLA Ops:
  7.2 1.4 fusion
  9.2 6.4 %all-to-all-start = ((f32[8,1,128]{2,1,0:T(1,128)}), f32[8,1,128]{2,1,0:T(1,128)S(1)}, u32[]{:S(2)}, u32[]{:S(2)}) async-start(f32[8,1,128]{2,1,0:T(1,128)} %broadcast_in_dim.14), calls=%async_computation | async-start | bytes 8192 | tf_op jit(solution)/shard_map/all_to_all | solution.py:16
  15.6 0.7 convert_element_type.52
  16.3 4.2 %all-to-all-done = f32[8,1,128]{2,1,0:T(1,128)S(1)} async-done(((f32[8,1,128]{2,1,0:T(1,128)}), f32[8,1,128]{2,1,0:T(1,128)S(1)}, u32[]{:S(2)}, u32[]{:S(2)}) %all-to-all-start) | async-done | bytes 4128 | tf_op jit(solution)/shard_map/all_to_all | solution.py:16
  20.5 2.0 fusion.2
  22.6 107.4 %all-gather.3.cloned.1.call-done = bf16[4096,2048]{1,0:T(8,128)(2,1)} async-done(((bf16[128,2048]{1,0:T(8,128)(2,1)}), bf16[4096,2048]{1,0:T(8,128)(2,1)}) %all-gather.3.cloned.1.call-update) | async-done | bytes 16777232 | tf_op jit(solution)/shard_map/all_gather | solution.py:66
  130.0 10.9 %convolution_convert_fusion.1 = bf16[4096,64]{0,1:T(8,128)(2,1)S(1)} fusion(bf16[4096,2048]{1,0:T(8,128)(2,1)} %all-gather.3.cloned.1.call-done, bf16[2048,64]{0,1:T(8,128)(2,1)} %param.9), kind=kOutput, calls=%fused_computation.2 | convolution fusion | flops 1074003968 | bytes 17563648 | tf_op jit(solution)/shard_map/dot_general | solution.py:71
  140.9 0.8 copy.51
  141.8 18.8 %all-to-all-start.2 = ((bf16[8,512,64]{1,2,0:T(8,128)(2,1)}), bf16[8,512,64]{1,2,0:T(8,128)(2,1)S(1)}, u32[]{:S(2)}, u32[]{:S(2)}) async-start(bf16[8,512,64]{1,2,0:T(8,128)(2,1)} %bitcast.22), calls=%async_computation.2 | async-start | bytes 1048576 | tf_op jit(solution)/shard_map/all_to_all | solution.py:31
  160.6 13.7 %convolution_convert_fusion = bf16[4096,512]{1,0:T(8,128)(2,1)} fusion(bf16[4096,2048]{1,0:T(8,128)(2,1)} %all-gather.3.cloned.1.call-done, bf16[2048,512]{1,0:T(8,128)(2,1)S(1)} %copy-done), kind=kOutput, calls=%fused_computation.1 | convolution fusion | flops 8592031744 | bytes 23068672 | tf_op jit(solution)/shard_map/dot_general | solution.py:68
  174.4 5.3 %all-to-all-start.1 = ((bf16[8,512,512]{2,1,0:T(8,128)(2,1)}), bf16[8,512,512]{2,1,0:T(8,128)(2,1)}, u32[]{:S(2)}, u32[]{:S(2)}) async-start(bf16[8,512,512]{2,1,0:T(8,128)(2,1)} %bitcast.23), calls=%async_computation.1 | async-start | bytes 8388608 | tf_op jit(solution)/shard_map/all_to_all | solution.py:31
  180.9 0.7 select_convert_fusion
  181.7 57.3 %all-gather.5.cloned.1.call-done = bf16[512,2048]{0,1:T(8,128)(2,1)} async-done(((bf16[512,64]{0,1:T(8,128)(2,1)}), bf16[512,2048]{0,1:T(8,128)(2,1)}) %all-gather.5.cloned.1.call-update) | async-done | bytes 2097168 | tf_op jit(solution)/shard_map/all_gather | solution.py:82
  239.0 4.6 %copy.40 = bf16[512,8,256]{2,1,0:T(8,128)(2,1)} copy(bf16[512,8,256]{0,2,1:T(8,128)(2,1)} %bitcast.25) | data formatting | bytes 4194304 | tf_op jit(solution)/shard_map/reshape | solution.py:85
  243.6 2.3 convolution_convert_fusion.2
  245.9 0.9 copy.39
  246.8 2.9 %convert_reduce_fusion = f32[512,512]{1,0:T(8,128)S(1)} fusion(bf16[8,512,512]{2,1,0:T(8,128)(2,1)} %all-to-all-done.1), kind=kLoop, calls=%fused_computation | loop fusion | flops 3932160 | bytes 5242880 | tf_op jit(solution)/shard_map/reduce_sum | solution.py:32
  249.7 1.3 copy.29
  251.0 1.8 reshape.312
  252.8 1.8 fusion.24
  254.6 1.2 copy.41
  255.9 1.2 copy.42
  257.1 2.4 fusion.8
  260.3 1.0 copy.38
  (32 shorter events, 2.7 us)
Async XLA Ops:
  7.2 153.5 %copy-start = (bf16[2048,512]{1,0:T(8,128)(2,1)S(1)}, bf16[2048,512]{1,0:T(8,128)(2,1)}, u32[]{:S(2)}) copy-start(bf16[2048,512]{1,0:T(8,128)(2,1)} %param.8) | copy-start | bytes 6291460
  9.2 11.3 %all-to-all-start = ((f32[8,1,128]{2,1,0:T(1,128)}), f32[8,1,128]{2,1,0:T(1,128)S(1)}, u32[]{:S(2)}, u32[]{:S(2)}) async-start(f32[8,1,128]{2,1,0:T(1,128)} %broadcast_in_dim.14), calls=%async_computation | async-start | bytes 8192 | tf_op jit(solution)/shard_map/all_to_all | solution.py:16
  15.5 114.5 %all-gather.3.cloned.1.call-start = ((), (), s32[]{:S(2)}) async-start(), calls=%async_computation.3 | async-start | bytes 17301504 | tf_op jit(solution)/shard_map/all_gather | solution.py:66
  141.8 32.6 %all-to-all-start.2 = ((bf16[8,512,64]{1,2,0:T(8,128)(2,1)}), bf16[8,512,64]{1,2,0:T(8,128)(2,1)S(1)}, u32[]{:S(2)}, u32[]{:S(2)}) async-start(bf16[8,512,64]{1,2,0:T(8,128)(2,1)} %bitcast.22), calls=%async_computation.2 | async-start | bytes 1048576 | tf_op jit(solution)/shard_map/all_to_all | solution.py:31
  174.4 5.5 %copy-start.1 = (s32[512]{0:T(512)S(1)}, s32[512]{0:T(512)}, u32[]{:S(2)}) copy-start(s32[512]{0:T(512)} %param.10) | copy-start | bytes 6148
  174.4 7.3 %copy-start.2 = (s32[8]{0:T(128)S(1)}, s32[8]{0:T(128)}, u32[]{:S(2)}) copy-start(s32[8]{0:T(128)} %param.11) | copy-start | bytes 100
  174.4 72.4 %all-to-all-start.1 = ((bf16[8,512,512]{2,1,0:T(8,128)(2,1)}), bf16[8,512,512]{2,1,0:T(8,128)(2,1)}, u32[]{:S(2)}, u32[]{:S(2)}) async-start(bf16[8,512,512]{2,1,0:T(8,128)(2,1)} %bitcast.23), calls=%async_computation.1 | async-start | bytes 8388608 | tf_op jit(solution)/shard_map/all_to_all | solution.py:31
  179.6 59.4 %all-gather.5.cloned.1.call-start = ((), (), s32[]{:S(2)}) async-start(), calls=%async_computation.4 | async-start | bytes 2162688 | tf_op jit(solution)/shard_map/all_gather | solution.py:82
Sparse Core Ops, SparseCore 0:
  22.7 107.2 all-gather.2
  183.6 55.3 all-gather.4
where the time goes:
time: 269 us; the launch traced here: 268 us
  waiting for transfers between devices  169 us (63%)
  starting transfers between devices  30.7 us (11%)
  matrix products  27 us (10%)
  local copies, waits for them, and re-layouts  16.5 us (6%)
  between operations  14.2 us (5%)
  other arithmetic  10.6 us (4%)
    all_gather x1, waiting for transfers between devices, body(): gathered = lax.all_gather(normed_rows, ('gx', 'gy'), axis=0, tiled=True)  107 us
    all_gather x1, waiting for transfers between devices, body(): keyval_all = lax.all_gather(keyval_part, ('gx', 'gy'), axis=1, tiled=True)  57.3 us
    all_to_all x2, starting transfers between devices, summed_on_arrival(): lax.all_to_all(in_blocks(value, dim, count), axis, 0, 0, tiled=True)  24.1 us
    dot_general x1, matrix products, body(): jnp.dot(gathered, w_query, preferred_element_type=jnp.float32)  13.7 us
    dot_general x1, matrix products, body(): jnp.dot(gathered, w_keyval, preferred_element_type=jnp.float32)  10.9 us
    all_to_all x1, starting transfers between devices, from_everyone(): return lax.all_to_all(copies, axis, split_axis=0, concat_axis=0, tiled=True)  6.36 us
  transfers between devices with their start and end apart: 5, of which 3 were waited for; matrix products, arithmetic and copies ran while one was open for 9% of the time, Pallas kernels for 0%

commit v1 on v0

--- a/solution.py
+++ b/solution.py
@@ -63,7 +63,10 @@
     query_width = w_query.shape[1]
     keyval_width = w_keyval.shape[1]
     group_size = lax.axis_size("gy")
-    gathered = lax.all_gather(normed_rows, ("gx", "gy"), axis=0, tiled=True)
+    gathered = jnp.concatenate(
+        lax.all_to_all(jnp.stack([normed_rows] * lax.axis_size(("gx", "gy"))), ("gx", "gy"), 0, 0),
+        axis=0,
+    )
     query_sum = summed_on_arrival(
         jnp.dot(gathered, w_query, preferred_element_type=jnp.float32).astype(jnp.bfloat16), "gz", 0
     )

time: 269 us -> 526 us (1.96)
  blocking collectives: 0 us -> 378 us
  waiting for transfers between devices: 169 us -> 63.3 us
  starting transfers between devices: 30.7 us -> 15.3 us
  local copies, waits for them, and re-layouts: 16.5 us -> 23.1 us
  matrix products: 27 us -> 21.3 us
    all_to_all x0 -> x1, blocking collectives: none -> 378 us  [body(): lax.all_to_all(jnp.stack([normed_rows] * lax.axis_size(('gx', 'gy'))), ('...]
    all_gather x1 -> x0, waiting for transfers between devices: 107 us -> none  [body(): gathered = lax.all_gather(normed_rows, ('gx', 'gy'), axis=0, tiled=True)]
    all_to_all x2, starting transfers between devices: 24.1 us -> 8.7 us  [summed_on_arrival(): lax.all_to_all(in_blocks(value, dim, count), axis, 0, 0, tiled=True)]
    another operation x0 -> x1, local copies, waits for them, and re-layouts: none -> 5.99 us  [body(): jnp.stack([normed_rows] * lax.axis_size(('gx', 'gy')))]
    dot_general x1, matrix products: 10.9 us -> 5.17 us  [body(): jnp.dot(gathered, w_keyval, preferred_element_type=jnp.float32)]
  transfers between devices with their start and end apart: 5 -> 4, of which waited for: 3 -> 2; matrix products, arithmetic and copies ran while one was open for 9% -> 5% of each run, Pallas kernels for 0% -> 0%
where the time goes in v1:
time: 526 us; the launch traced here: 525 us
  blocking collectives  378 us (72%)
  waiting for transfers between devices  63.3 us (12%)
  local copies, waits for them, and re-layouts  23.1 us (4%)
  matrix products  21.3 us (4%)
  starting transfers between devices  15.3 us (3%)
  between operations  14.2 us (3%)
  other arithmetic  9.8 us (2%)
    all_to_all x1, blocking collectives, body(): lax.all_to_all(jnp.stack([normed_rows] * lax.axis_size(('gx', 'gy'))), ('...  378 us
    all_gather x1, waiting for transfers between devices, body(): keyval_all = lax.all_gather(keyval_part, ('gx', 'gy'), axis=1, tiled=True)  59 us
    dot_general x1, matrix products, body(): jnp.dot(gathered, w_query, preferred_element_type=jnp.float32)  13.7 us
  transfers between devices with their start and end apart: 4, of which 2 were waited for; matrix products, arithmetic and copies ran while one was open for 5% of the time, Pallas kernels for 0%

profile of v1, /device:TPU:1, one launch (start us, length us, event | category | flops | bytes accessed | tf_op | source)
XLA Modules:
  0.0 525.3 jit_solution(15483415424193471161)
XLA Ops:
  7.2 1.4 fusion
  9.2 6.4 %all-to-all-start = ((f32[8,1,128]{2,1,0:T(1,128)}), f32[8,1,128]{2,1,0:T(1,128)S(1)}, u32[]{:S(2)}, u32[]{:S(2)}) async-start(f32[8,1,128]{2,1,0:T(1,128)} %broadcast_in_dim.14), calls=%async_computation | async-start | bytes 8192 | tf_op jit(solution)/shard_map/all_to_all | solution.py:16
  16.2 4.3 all-to-all-done
  20.5 1.2 fusion.2
  21.7 6.0 %stack.9 = bf16[32,128,2048]{2,1,0:T(8,128)(2,1)} broadcast(bf16[128,2048]{1,0:T(8,128)(2,1)S(1)} %fusion.2), dimensions={1,2} | broadcast | bytes 17301504 | tf_op jit(solution)/shard_map/stack | solution.py:67
  27.7 378.3 %all_to_all.21 = bf16[32,128,2048]{2,1,0:T(8,128)(2,1)S(1)} all-to-all(bf16[32,128,2048]{2,1,0:T(8,128)(2,1)} %stack.9), channel_id=1, replica_groups=mesh['gx'=8,'gy'=4,'gz'=8] {'gx','gy'}, dimensions={0} | all-to-all | bytes 33554432 | tf_op jit(solution)/shard_map/all_to_all | solution.py:67
  406.0 5.2 convolution_convert_fusion.1
  411.8 0.8 copy.51
  412.6 3.5 all-to-all-start.3
  416.1 13.7 %convolution_convert_fusion = bf16[4096,512]{1,0:T(8,128)(2,1)} fusion(bf16[4096,2048]{1,0:T(8,128)(2,1)} %bitcast.25, bf16[2048,512]{1,0:T(8,128)(2,1)S(1)} %copy-done), kind=kOutput, calls=%fused_computation.1 | convolution fusion | flops 8592031744 | bytes 23068672 | tf_op jit(solution)/shard_map/dot_general | solution.py:71
  429.9 5.2 all-to-all-start.2
  436.3 0.7 select_convert_fusion
  437.2 59.0 %all-gather.2.cloned.1.call-done = bf16[512,2048]{0,1:T(8,128)(2,1)} async-done(((bf16[512,64]{0,1:T(8,128)(2,1)}), bf16[512,2048]{0,1:T(8,128)(2,1)}) %all-gather.2.cloned.1.call-update) | async-done | bytes 2097168 | tf_op jit(solution)/shard_map/all_gather | solution.py:85
  496.2 4.6 copy.40
  500.7 2.3 convolution_convert_fusion.2
  503.1 0.9 copy.39
  503.9 2.9 convert_reduce_fusion
  506.8 1.3 copy.29
  508.1 1.8 reshape.318
  510.0 1.8 fusion.24
  511.8 1.2 copy.42
  513.0 1.2 copy.41
  514.3 2.4 fusion.8
  517.4 1.0 copy.38
  (35 shorter events, 3.9 us)
Async XLA Ops:
  7.2 408.9 %copy-start = (bf16[2048,512]{1,0:T(8,128)(2,1)S(1)}, bf16[2048,512]{1,0:T(8,128)(2,1)}, u32[]{:S(2)}) copy-start(bf16[2048,512]{1,0:T(8,128)(2,1)} %param.8) | copy-start | bytes 6291460
  9.2 11.3 %all-to-all-start = ((f32[8,1,128]{2,1,0:T(1,128)}), f32[8,1,128]{2,1,0:T(1,128)S(1)}, u32[]{:S(2)}, u32[]{:S(2)}) async-start(f32[8,1,128]{2,1,0:T(1,128)} %broadcast_in_dim.14), calls=%async_computation | async-start | bytes 8192 | tf_op jit(solution)/shard_map/all_to_all | solution.py:16
  27.7 378.3 %copy-start.2 = (bf16[2048,64]{0,1:T(8,128)(2,1)S(1)}, bf16[2048,64]{0,1:T(8,128)(2,1)}, u32[]{:S(2)}) copy-start(bf16[2048,64]{0,1:T(8,128)(2,1)} %param.9) | copy-start | bytes 786436
  406.0 5.7 %copy-start.1 = (bf16[32,128,2048]{2,1,0:T(8,128)(2,1)}, bf16[32,128,2048]{2,1,0:T(8,128)(2,1)S(1)}, u32[]{:S(2)}) copy-start(bf16[32,128,2048]{2,1,0:T(8,128)(2,1)S(1)} %all_to_all.21) | copy-start | bytes 50331652
  412.6 17.3 %all-to-all-start.3 = ((bf16[8,512,64]{1,2,0:T(8,128)(2,1)}), bf16[8,512,64]{1,2,0:T(8,128)(2,1)S(1)}, u32[]{:S(2)}, u32[]{:S(2)}) async-start(bf16[8,512,64]{1,2,0:T(8,128)(2,1)} %bitcast.23), calls=%async_computation.3 | async-start | bytes 1048576 | tf_op jit(solution)/shard_map/all_to_all | solution.py:31
  429.9 5.4 %copy-start.3 = (s32[512]{0:T(512)S(1)}, s32[512]{0:T(512)}, u32[]{:S(2)}) copy-start(s32[512]{0:T(512)} %param.10) | copy-start | bytes 6148
  429.9 7.2 %copy-start.4 = (s32[8]{0:T(128)S(1)}, s32[8]{0:T(128)}, u32[]{:S(2)}) copy-start(s32[8]{0:T(128)} %param.11) | copy-start | bytes 100
  429.9 74.1 %all-to-all-start.2 = ((bf16[8,512,512]{2,1,0:T(8,128)(2,1)}), bf16[8,512,512]{2,1,0:T(8,128)(2,1)}, u32[]{:S(2)}, u32[]{:S(2)}) async-start(bf16[8,512,512]{2,1,0:T(8,128)(2,1)} %bitcast.26), calls=%async_computation.2 | async-start | bytes 8388608 | tf_op jit(solution)/shard_map/all_to_all | solution.py:31
  435.1 61.1 %all-gather.2.cloned.1.call-start = ((), (), s32[]{:S(2)}) async-start(), calls=%async_computation.4 | async-start | bytes 2162688 | tf_op jit(solution)/shard_map/all_gather | solution.py:85
Sparse Core Ops, SparseCore 0:
  439.0 57.0 all-gather.1
